TPU v7x, 32 devices: a whole 2x2x4 slice. The times are simulated.
32 devices in a mesh: dp: 2 (over y), row: 4 (over x, core), col: 4 (over z).
Axes of the slice: x: 2, y: 2, z: 4, core: 2. Of those that a mesh axis runs over, the one named last changes fastest.
Arguments:
- tokens: bfloat16 [2048, 8192], P(('dp', 'col'), 'row'), may hold values from -6 to 6
- frozen_weight: bfloat16 [8192, 8192], P('row', 'col'), may hold values from -0.0625 to 0.0625
- input_adapter_factor: bfloat16 [16, 8192], P(None, 'row'), may hold values from -0.0625 to 0.0625
- output_adapter_factor: bfloat16 [16, 8192], P(None, 'col'), may hold values from -1.5 to 1.5
- magnitude: float32 [8192], P('col'), may hold values from 0.5 to 2
- cotangent: bfloat16 [2048, 8192], P(('dp', 'row'), 'col'), may hold values from -6 to 6
- sequence_lengths: int32 [2, 8], P('dp'), may hold values from 1 to 512, 1024 in all within a row
Outputs:
- projected: bfloat16 [2048, 8192], P(('dp', 'row'), 'col')
- grad_mag: float32 [8192], P('col')
- input_factor_gradient: float32 [16, 8192], P(None, 'row')
- grad_b: float32 [16, 8192], P(None, 'col')
Inputs may be any that keep to these rules, and one draw needn't show every extreme that they name: `sequence_lengths`: each group's 8 lengths sum to 1024, and one of them is exactly 512.
All inputs are finite; a program needn't handle non-finite values.
Results may differ from a plain program's by a relative error of at most 0.0052.
Values may be sent and summed in bfloat16 or wider, within the bound.
A program may use at most 64 MiB of HBM per device.

v0:
```python
import jax
import jax.numpy as jnp
from jax import lax
from jax.sharding import PartitionSpec as P

norm_eps = 1e-06
highest_precision = lax.Precision.HIGHEST


def contract_product(left, right, left_dim, right_dim):
    return lax.dot_general(
        left, right, (((left_dim,), (right_dim,)), ((), ())), preferred_element_type=jnp.float32
    )


def per_device(
    tokens,
    frozen_weight,
    input_adapter_factor,
    output_adapter_factor,
    magnitude,
    cotangent,
    sequence_lengths,
):
    row_count = lax.axis_size("row")
    col_count = lax.axis_size("col")
    row_index = lax.axis_index("row")
    col_index = lax.axis_index("col")
    group_index = lax.axis_index("dp")
    local_rows = tokens.shape[0]
    group_rows = local_rows * col_count
    block_rows = group_rows // row_count
    adapter_rank_size = input_adapter_factor.shape[0]
    low_rank_update = contract_product(input_adapter_factor, output_adapter_factor, 0, 0)
    merged = frozen_weight.astype(jnp.float32) + low_rank_update
    norm_terms = jnp.sum(merged * merged, axis=0)
    gram_partial_terms = contract_product(input_adapter_factor, input_adapter_factor, 1, 1)
    merged_factor_terms = jnp.dot(
        input_adapter_factor, frozen_weight, preferred_element_type=jnp.float32
    ) + jnp.dot(
        gram_partial_terms, output_adapter_factor.astype(jnp.float32), precision=highest_precision
    )
    portion = lax.all_gather(tokens, "col", axis=0, tiled=True)
    base_piece = jnp.dot(portion, frozen_weight, preferred_element_type=jnp.float32)
    down_portion = contract_product(portion, input_adapter_factor, 1, 1)
    frozen_rows, down_rows = (
        lax.psum_scatter(base_piece, "row", scatter_dimension=0, tiled=True),
        lax.psum_scatter(down_portion, "row", scatter_dimension=0, tiled=True),
    )
    norm_sq, merged_input_factor = lax.psum((norm_terms, merged_factor_terms), "row")
    down_activations = down_rows.astype(jnp.bfloat16)
    col_norm = jnp.sqrt(norm_sq + norm_eps)
    col_scale = magnitude / col_norm
    query_projection = frozen_rows + jnp.dot(
        down_activations, output_adapter_factor, preferred_element_type=jnp.float32
    )
    projected = (query_projection * col_scale[None, :]).astype(jnp.bfloat16)
    lengths = sequence_lengths[0]
    ends = jnp.cumsum(lengths, dtype=jnp.int32)
    starts = ends - lengths
    positions = row_index * block_rows + jnp.arange(block_rows, dtype=jnp.int32)
    inside = (positions[:, None] >= starts[None, :]) & (positions[:, None] < ends[None, :])
    inverse = 1.0 / lengths.astype(jnp.float32)
    weights = jnp.sum(jnp.where(inside, inverse[None, :], jnp.float32(0.0)), axis=1)
    grad_out = cotangent.astype(jnp.float32) * weights[:, None]
    scale_terms = jnp.sum(grad_out * query_projection, axis=0)
    projection_gradient = (grad_out * col_scale[None, :]).astype(jnp.bfloat16)
    bgrad_terms = contract_product(down_activations, projection_gradient, 0, 0)
    scale_grad, bgrad_data = lax.psum((scale_terms, bgrad_terms), ("dp", "row"))
    grad_mag = scale_grad / col_norm
    norm_coefficient = -scale_grad * magnitude / (col_norm * col_norm * col_norm)
    grad_b = bgrad_data + merged_input_factor * norm_coefficient[None, :]
    backward_terms = contract_product(projection_gradient, output_adapter_factor, 1, 1)
    padded = lax.dynamic_update_slice_in_dim(
        jnp.zeros((group_rows, adapter_rank_size), jnp.float32),
        backward_terms,
        row_index * block_rows,
        0,
    )
    backward_rows = lax.psum(padded, ("row", "col")).astype(jnp.bfloat16)
    back_mine = lax.dynamic_slice_in_dim(backward_rows, col_index * local_rows, local_rows, 0)
    row_term = contract_product(back_mine, tokens, 0, 0)
    scaled_output_factor = (
        output_adapter_factor.astype(jnp.float32) * norm_coefficient[None, :]
    ).astype(jnp.bfloat16)
    norm_term = contract_product(scaled_output_factor, frozen_weight, 1, 1) + jnp.dot(
        contract_product(scaled_output_factor, output_adapter_factor, 1, 1),
        input_adapter_factor.astype(jnp.float32),
        precision=highest_precision,
    )
    first_group = (group_index == 0).astype(jnp.float32)
    input_factor_gradient = lax.psum(row_term + first_group * norm_term, ("dp", "col"))
    return (projected, grad_mag, input_factor_gradient, grad_b)


def solution(mesh):
    in_specs = (
        P(("dp", "col"), "row"),
        P("row", "col"),
        P(None, "row"),
        P(None, "col"),
        P("col"),
        P(("dp", "row"), "col"),
        P("dp", None),
    )
    out_specs = (P(("dp", "row"), "col"), P("col"), P(None, "row"), P(None, "col"))
    return jax.shard_map(
        per_device, mesh=mesh, in_specs=in_specs, out_specs=out_specs, check_vma=False
    )
```

profile of v0, /device:TPU:0, one launch (start us, length us, event | category | flops | bytes accessed | tf_op | source)
XLA Modules:
  0.0 366.2 jit_solution(13270679273868545477)
XLA Ops:
  7.2 0.0 copy-start
  7.2 0.0 all-gather.2.cloned.1.call-start
  7.2 0.7 all-gather.2.cloned.1.call-update
  7.9 0.0 reduce-scatter.5.cloned.1.call-start
  8.0 85.1 %all-gather.2.cloned.1.call-done = bf16[1024,2048]{1,0:T(8,128)(2,1)} async-done(((bf16[256,2048]{1,0:T(8,128)(2,1)}), bf16[1024,2048]{1,0:T(8,128)(2,1)}) %all-gather.2.cloned.1.call-update) | async-done | bytes 4194320 | tf_op jit(solution)/shard_map/all_gather | solution.py:43
  93.1 0.0 copy-done
  93.1 4.0 %fusion.14 = f32[1024,16]{0,1:T(8,128)} fusion(bf16[1024,2048]{1,0:T(8,128)(2,1)} %all-gather.2.cloned.1.call-done, bf16[16,2048]{1,0:T(8,128)(2,1)S(1)} %copy-done), kind=kOutput, calls=%fused_computation.33 | convolution fusion | flops 67108864 | bytes 4325376 | tf_op jit(solution)/shard_map/dot_general | solution.py:11
  97.1 0.0 reduce-scatter.5.cloned.1.call-update
  97.1 0.0 reduce-scatter.3.cloned.1.call-start
  97.1 14.4 %fusion.13 = f32[1024,2048]{1,0:T(8,128)} fusion(bf16[1024,2048]{1,0:T(8,128)(2,1)} %all-gather.2.cloned.1.call-done, bf16[2048,2048]{1,0:T(8,128)(2,1)} %param.8), kind=kOutput, calls=%fused_computation.32 | convolution fusion | flops 8589934592 | bytes 20971520 | tf_op jit(solution)/shard_map/dot_general | solution.py:44
  111.6 0.0 reduce-scatter.3.cloned.1.call-update
  111.6 0.0 all-reduce.8.cloned.1.call-start
  111.6 0.1 fusion.16
  111.8 4.6 %fusion.15 = f32[16,2048]{1,0:T(8,128)S(1)} fusion(bf16[16,2048]{1,0:T(8,128)(2,1)S(1)} %copy-done, bf16[2048,2048]{1,0:T(8,128)(2,1)} %param.8), kind=kOutput, calls=%fused_computation.34 | convolution fusion | flops 134217728 | bytes 8585216 | tf_op jit(solution)/shard_map/dot_general | solution.py:38
  116.4 0.0 copy-done.2
  116.4 0.9 convolution_add_fusion.1
  117.3 0.0 all-reduce.8.cloned.1.call-update
  117.3 0.0 all-reduce.6.cloned.1.call-start
  117.3 0.0 copy-start.5
  117.4 0.0 copy-start.4
  117.4 0.0 copy-start.3
  117.4 5.9 %multiply_reduce_fusion = f32[2048]{0:T(1024)S(1)} fusion(bf16[2048,2048]{1,0:T(8,128)(2,1)} %param.8, bf16[16,2048]{1,0:T(8,128)(2,1)S(1)} %copy-done, bf16[16,2048]{1,0:T(8,128)(2,1)S(1)} %copy-done.2), kind=kOutput, calls=%fused_computation | convolution fusion | flops 150992896 | bytes 8527872 | tf_op jit(solution)/shard_map/dot_general | solution.py:11
  123.3 0.0 copy-done.5
  123.3 0.2 reduce-window.4
  123.5 6.5 %psum.42 = f32[2048]{0:T(1024)S(1)} all-reduce(f32[2048]{0:T(1024)S(1)} %multiply_reduce_fusion), channel_id=1, replica_groups=mesh['dp'=2,'row'=4,'col'=4] {'row'}, use_global_device_ids=true, to_apply=%region_3.0 | all-reduce | flops 2048 | bytes 16384 | tf_op jit(solution)/shard_map/psum | solution.py:50
  130.0 0.0 copy-done.4
  130.1 0.1 select_reduce_fusion
  130.2 0.5 convolution_dynamic-update-slice_fusion
  130.7 69.2 %psum.44 = bf16[1024,16]{1,0:T(8,128)(2,1)S(1)} all-reduce(f32[1024,16]{1,0:T(8,128)S(1)} %convolution_dynamic-update-slice_fusion), channel_id=1, replica_groups=mesh['dp'=2,'row'=4,'col'=4] {'row','col'}, use_global_device_ids=true, to_apply=%region_8.9 | all-reduce | flops 16384 | bytes 98304 | tf_op jit(solution)/shard_map/psum | solution.py:80
  199.9 0.0 reduce-scatter.5.cloned.1.call-done
  200.0 1.8 fusion.1
  201.8 0.0 all-reduce.6.cloned.1.call-update
  201.8 0.0 all-reduce.4.cloned.1.call-start
  201.8 0.0 reduce-scatter.3.cloned.1.call-done
  201.9 3.2 multiply_reduce_fusion.1
  205.1 12.1 %psum.43 = f32[2048]{0:T(1024)S(1)} all-reduce(f32[2048]{0:T(1024)S(1)} %get-tuple-element.4), channel_id=1, replica_groups=mesh['dp'=2,'row'=4,'col'=4] {'dp','row'}, use_global_device_ids=true, to_apply=%region_7.8 | all-reduce | flops 2048 | bytes 16384 | tf_op jit(solution)/shard_map/psum | solution.py:69
  217.1 0.6 fusion.6
  217.8 5.7 %fusion.3 = f32[16,2048]{1,0:T(8,128)S(1)} fusion(bf16[2048,2048]{1,0:T(8,128)(2,1)} %param.8, bf16[16,2048]{1,0:T(8,128)(2,1)S(1)} %copy-done.2, f32[2048]{0:T(1024)S(1)} %get-tuple-element.6), kind=kOutput, calls=%fused_computation.16 | convolution fusion | flops 134316032 | bytes 8593408 | tf_op jit(solution)/shard_map/dot_general | solution.py:11
  223.5 0.1 fusion.2
  223.6 0.2 fusion
  223.9 0.0 copy-done.1
  223.9 0.9 convolution_add_fusion.3
  224.8 0.0 all-reduce.4.cloned.1.call-update
  224.8 2.4 all-reduce.8.cloned.1.call-done
  227.2 57.0 %all-reduce.6.cloned.1.call-done = f32[16,2048]{1,0:T(8,128)} async-done(((f32[16,2048]{1,0:T(8,128)}), f32[16,2048]{1,0:T(8,128)}) %all-reduce.6.cloned.1.call-update) | async-done | bytes 131088 | tf_op jit(solution)/shard_map/psum | solution.py:69
  284.2 1.6 multiply_add_fusion
  285.9 71.9 %all-reduce.4.cloned.1.call-done = f32[16,2048]{1,0:T(8,128)} async-done(((f32[16,2048]{1,0:T(8,128)}), f32[16,2048]{1,0:T(8,128)}) %all-reduce.4.cloned.1.call-update) | async-done | bytes 131088 | tf_op jit(solution)/shard_map/psum | solution.py:92
  357.8 1.6 copy.15
  (8 shorter events, 0.1 us)
Async XLA Ops:
  7.2 85.9 %copy-start = (bf16[16,2048]{1,0:T(8,128)(2,1)S(1)}, bf16[16,2048]{1,0:T(8,128)(2,1)}, u32[]{:S(2)}) copy-start(bf16[16,2048]{1,0:T(8,128)(2,1)} %param.9) | copy-start | bytes 196612
  7.2 85.9 %all-gather.2.cloned.1.call-start = ((), (), s32[]{:S(2)}) async-start(), calls=%async_computation.2 | async-start | bytes 5242880 | tf_op jit(solution)/shard_map/all_gather | solution.py:43
  7.9 192.0 %reduce-scatter.5.cloned.1.call-start = ((), (), s32[]{:S(2)}) async-start(), calls=%async_computation.4 | async-start | bytes 81920 | tf_op jit(solution)/shard_map/reduce_scatter | solution.py:48
  97.1 104.8 %reduce-scatter.3.cloned.1.call-start = ((), (), s32[]{:S(2)}) async-start(), calls=%async_computation.3 | async-start | bytes 10485760 | tf_op jit(solution)/shard_map/reduce_scatter | solution.py:47
  111.6 115.7 %all-reduce.8.cloned.1.call-start = ((), (), s32[]{:S(2)}) async-start(), calls=%async_computation.7 | async-start | bytes 262144 | tf_op jit(solution)/shard_map/psum | solution.py:50
  111.8 4.6 %copy-start.2 = (bf16[16,2048]{1,0:T(8,128)(2,1)S(1)}, bf16[16,2048]{1,0:T(8,128)(2,1)}, u32[]{:S(2)}) copy-start(bf16[16,2048]{1,0:T(8,128)(2,1)} %param.10) | copy-start | bytes 196612
  117.3 166.9 %all-reduce.6.cloned.1.call-start = ((), (), s32[]{:S(2)}) async-start(), calls=%async_computation.6 | async-start | bytes 262144 | tf_op jit(solution)/shard_map/psum | solution.py:69
  117.3 5.9 %copy-start.5 = (s32[1,8]{1,0:T(1,128)S(1)}, s32[1,8]{1,0:T(1,128)}, u32[]{:S(2)}) copy-start(s32[1,8]{1,0:T(1,128)} %param.13) | copy-start | bytes 100
  117.4 12.7 %copy-start.4 = (f32[2048]{0:T(1024)S(1)}, f32[2048]{0:T(1024)}, u32[]{:S(2)}) copy-start(f32[2048]{0:T(1024)} %param.11) | copy-start | bytes 24580
  117.4 12.8 %copy-start.3 = (bf16[256,2048]{1,0:T(8,128)(2,1)S(1)}, bf16[256,2048]{1,0:T(8,128)(2,1)}, u32[]{:S(2)}) copy-start(bf16[256,2048]{1,0:T(8,128)(2,1)} %param.12) | copy-start | bytes 3145732
  201.8 156.0 %all-reduce.4.cloned.1.call-start = ((), (), s32[]{:S(2)}) async-start(), calls=%async_computation.5 | async-start | bytes 262144 | tf_op jit(solution)/shard_map/psum | solution.py:92
  217.8 6.1 %copy-start.1 = (bf16[256,2048]{1,0:T(8,128)(2,1)S(1)}, bf16[256,2048]{1,0:T(8,128)(2,1)}, u32[]{:S(2)}) copy-start(bf16[256,2048]{1,0:T(8,128)(2,1)} %param.7) | copy-start | bytes 3145732
Sparse Core Ops, SparseCore 0:
  9.6 83.4 all-gather.1
  97.2 18.0 reduce-scatter.4
  117.9 75.6 reduce-scatter.2
  195.8 31.4 all-reduce.7
  230.7 53.4 all-reduce.5
  288.0 69.7 all-reduce.3
where the time goes:
time: 367 us; the launch traced here: 366 us
  waiting for transfers between devices  217 us (59%)
  blocking collectives  87.8 us (24%)
  matrix products  42.5 us (12%)
  between operations  14.3 us (4%)
    all_gather x1, waiting for transfers between devices, per_device(): portion = lax.all_gather(tokens, 'col', axis=0, tiled=True)  85.1 us
    psum x1, waiting for transfers between devices, per_device(): lax.psum(row_term + first_group * norm_term, ('dp', 'col'))  71.9 us
    psum x1, blocking collectives, per_device(): backward_rows = lax.psum(padded, ('row', 'col')).astype(jnp.bfloat16)  69.2 us
    psum x1, waiting for transfers between devices, per_device(): scale_grad, bgrad_data = lax.psum((scale_terms, bgrad_terms), ('dp', 'row'))  57 us
    dot_general x8, matrix products, contract_product(): lax.dot_general(left, right, (((left_dim,), (right_dim,)), ((), ())), pre...  19.1 us
    dot_general x1, matrix products, per_device(): jnp.dot(portion, frozen_weight, preferred_element_type=jnp.float32)  14.4 us
    psum x1, blocking collectives, per_device(): scale_grad, bgrad_data = lax.psum((scale_terms, bgrad_terms), ('dp', 'row'))  12.1 us
  transfers between devices with their start and end apart: 6, of which 4 were waited for; matrix products, arithmetic and copies ran while one was open for 11% of the time, Pallas kernels for 0%

commit v1 on v0

v1 whole, which is shorter than its diff:
```python
import functools

import jax
import jax.numpy as jnp
from jax import lax
from jax.experimental import pallas as pl
from jax.experimental.pallas import tpu as pltpu
from jax.sharding import PartitionSpec as P

norm_eps = 1e-06
highest_precision = lax.Precision.HIGHEST
MESH = pl.DeviceIdType.MESH
LANES = 128
VMEM_LIMIT = 60 * 1024 * 1024


def contract_product(left, right, left_dim, right_dim):
    return lax.dot_general(
        left, right, (((left_dim,), (right_dim,)), ((), ())), preferred_element_type=jnp.float32
    )


def column_tiles(width, tile):
    return [(start, min(tile, width - start)) for start in range(0, width, tile)]


def project_kernel(
    C, R, S,
    tok, w_hbm, at_hbm, a_ref, b_ref,
    q_out, g_out, stat_out,
    wx, gath, sb, pin, xin, pb, st_mine, st_in,
    load_sem, gsend, grecv, ssend, precv, xrecv, stsend, strecv,
):
    z = lax.axis_index("col")
    r = lax.axis_index("row")
    p, q = r // 2, r % 2
    pairs = R // 2
    sub, features = tok.shape[1], tok.shape[2]
    cols = w_hbm.shape[1]
    rank_rows = a_ref.shape[0]
    units = C * S
    block_units = units // R
    tiles = column_tiles(cols, 512)

    load_w = pltpu.make_async_copy(w_hbm, wx.at[:, pl.ds(0, cols)], load_sem.at[0])
    load_a = pltpu.make_async_copy(at_hbm, wx.at[:, pl.ds(cols, LANES)], load_sem.at[1])
    load_w.start()
    load_a.start()

    barrier = pltpu.get_barrier_semaphore()

    @pl.when(z > 0)
    def _():
        pl.semaphore_signal(barrier, inc=1, device_id={"col": z - 1}, device_id_type=MESH)

    @pl.when(z < C - 1)
    def _():
        pl.semaphore_signal(barrier, inc=1, device_id={"col": z + 1}, device_id_type=MESH)

    for i in range(1, R):
        pl.semaphore_signal(barrier, inc=1, device_id={"row": (r + i) % R}, device_id_type=MESH)

    @pl.when((z > 0) & (z < C - 1))
    def _():
        pl.semaphore_wait(barrier, R + 1)

    @pl.when((z == 0) | (z == C - 1))
    def _():
        pl.semaphore_wait(barrier, R)

    def hop(src, u, direction):
        target = z - 1 if direction == 0 else z + 1
        return pltpu.make_async_remote_copy(
            src_ref=src, dst_ref=gath.at[u], send_sem=gsend.at[direction, u],
            recv_sem=grecv.at[u], device_id={"col": target}, device_id_type=MESH,
        )

    for s in range(S):
        @pl.when(z > 0)
        def _():
            hop(tok.at[s], z * S + s, 0).start()

        @pl.when(z < C - 1)
        def _():
            hop(tok.at[s], z * S + s, 1).start()

    load_w.wait()
    load_a.wait()

    st_mine[...] = jnp.zeros_like(st_mine)
    a = a_ref[...]
    gram = contract_product(a, a, 1, 1)
    for start, width in tiles:
        span = pl.ds(start, width)
        st_mine[0:rank_rows, span] = jnp.dot(
            a, wx[:, span], preferred_element_type=jnp.float32
        ) + jnp.dot(
            gram, b_ref[0:rank_rows, span].astype(jnp.float32),
            precision=highest_precision, preferred_element_type=jnp.float32,
        )
    depth = 256

    def norm_step(i, carry):
        rows = pl.ds(pl.multiple_of(i * depth, depth), depth)
        for start, width in tiles:
            span = pl.ds(start, width)
            merged = wx[rows, span].astype(jnp.float32) + jnp.dot(
                wx[rows, pl.ds(cols, LANES)], b_ref[:, span], preferred_element_type=jnp.float32
            )
            st_mine[rank_rows:rank_rows + 1, span] += jnp.sum(merged * merged, axis=0, keepdims=True)
        return carry

    lax.fori_loop(0, features // depth, norm_step, 0)

    def stat_copy(i):
        return pltpu.make_async_remote_copy(
            src_ref=st_mine, dst_ref=st_in.at[i], send_sem=stsend.at[i], recv_sem=strecv.at[i],
            device_id={"row": (r + i) % R}, device_id_type=MESH,
        )

    near = jnp.minimum(z, C - 1 - z)

    def place(k):
        j = k - S
        both = j < 2 * near * S
        rest = j - 2 * near * S
        distance = jnp.where(both, j // (2 * S) + 1, near + 1 + rest // S)
        s = jnp.where(both, (j % (2 * S)) // 2, rest % S)
        leftward = jnp.where(both, j % 2 == 0, z > C - 1 - z)
        chunk = jnp.where(leftward, z - distance, z + distance)
        own = k < S
        return jnp.where(own, z, chunk), jnp.where(own, k, s)

    def pair_copy(u):
        return pltpu.make_async_remote_copy(
            src_ref=sb.at[u], dst_ref=pin.at[u], send_sem=ssend.at[u], recv_sem=precv.at[u],
            device_id={"row": p * 2 + (1 - q)}, device_id_type=MESH,
        )

    def far_copy(u, owner_pair):
        return pltpu.make_async_remote_copy(
            src_ref=sb.at[u], dst_ref=xin.at[p, u % block_units], send_sem=ssend.at[u],
            recv_sem=xrecv.at[p, u % block_units],
            device_id={"row": owner_pair * 2 + q}, device_id_type=MESH,
        )

    def multiply(k):
        c, s = place(k)
        u = c * S + s
        owner = u // block_units

        @pl.when(k < S)
        def _():
            gath[u] = tok[s]

        @pl.when(k >= S)
        def _():
            hop(gath.at[u], u, 0).wait_recv()

            @pl.when((c < z) & (z < C - 1))
            def _():
                hop(gath.at[u], u, 1).start()

            @pl.when((c > z) & (z > 0))
            def _():
                hop(gath.at[u], u, 0).start()

        slot = k % 2
        for start, width in column_tiles(cols + LANES, 512):
            span = pl.ds(start, width)
            pb[slot, :, span] = jnp.dot(gath[u], wx[:, span], preferred_element_type=jnp.float32)

        @pl.when(owner % 2 != q)
        def _():
            sb[u] = pb[slot].astype(jnp.bfloat16)
            pair_copy(u).start()

    def combine(k):
        c, s = place(k)
        u = c * S + s
        owner = u // block_units
        slot = k % 2

        @pl.when(owner % 2 == q)
        def _():
            pair_copy(u).wait_recv()
            total = pb[slot] + pin[u].astype(jnp.float32)

            @pl.when(owner // 2 == p)
            def _():
                q_out[u % block_units] = total

            @pl.when(owner // 2 != p)
            def _():
                sb[u] = total.astype(jnp.bfloat16)
                far_copy(u, owner // 2).start()

    def step(k, carry):
        @pl.when(k < units)
        def _():
            multiply(k)

        @pl.when(k == 0)
        def _():
            for i in range(1, R):
                stat_copy(i).start()

        @pl.when(k > 0)
        def _():
            combine(k - 1)

        return carry

    lax.fori_loop(0, units + 1, step, 0)

    keep = pltpu.make_async_copy(gath, g_out, load_sem.at[0])
    keep.start()
    for i in range(1, R):
        stat_copy(i).wait_recv()
    total = st_mine[...]
    for i in range(1, R):
        total = total + st_in[i]
    stat_out[...] = total

    def finish(v, carry):
        for i in range(1, pairs):
            other = (p + i) % pairs
            pltpu.make_async_remote_copy(
                src_ref=sb.at[v], dst_ref=xin.at[other, v], send_sem=ssend.at[v],
                recv_sem=xrecv.at[other, v], device_id={"row": other * 2 + q}, device_id_type=MESH,
            ).wait_recv()
            q_out[v] += xin[other, v].astype(jnp.float32)
        return carry

    lax.fori_loop(0, block_units, finish, 0)

    for i in range(1, R):
        stat_copy(i).wait_send()

    def drain(u, carry):
        c = u // S
        owner = u // block_units

        @pl.when((owner % 2 != q) | (owner // 2 != p))
        def _():
            pair_copy(u).wait_send()

        @pl.when((c <= z) & (z < C - 1))
        def _():
            hop(gath.at[u], u, 1).wait_send()

        @pl.when((c >= z) & (z > 0))
        def _():
            hop(gath.at[u], u, 0).wait_send()

        return carry

    lax.fori_loop(0, units, drain, 0)
    keep.wait()


def gather_project(tokens, frozen_weight, input_factor, output_factor):
    C, R = lax.axis_size("col"), lax.axis_size("row")
    local_rows, features = tokens.shape
    cols = frozen_weight.shape[1]
    rank_rows = input_factor.shape[0]
    S = 4
    sub = local_rows // S
    units = C * S
    block_units = units // R
    wide = cols + LANES
    stat_rows = rank_rows + 8
    at = jnp.pad(input_factor.T, ((0, 0), (0, LANES - rank_rows)))
    bp = jnp.pad(output_factor, ((0, LANES - rank_rows), (0, 0)))
    vmem = pl.BlockSpec(memory_space=pltpu.VMEM)
    hbm = pl.BlockSpec(memory_space=pl.ANY)
    dma = pltpu.SemaphoreType.DMA
    f32, bf16 = jnp.float32, jnp.bfloat16
    return pl.pallas_call(
        functools.partial(project_kernel, C, R, S),
        out_shape=(
            jax.ShapeDtypeStruct((block_units, sub, wide), f32),
            jax.ShapeDtypeStruct((units, sub, features), bf16),
            jax.ShapeDtypeStruct((stat_rows, cols), f32),
        ),
        in_specs=[vmem, hbm, hbm, vmem, vmem],
        out_specs=(vmem, hbm, vmem),
        scratch_shapes=[
            pltpu.VMEM((features, wide), bf16),
            pltpu.VMEM((units, sub, features), bf16),
            pltpu.VMEM((units, sub, wide), bf16),
            pltpu.VMEM((units, sub, wide), bf16),
            pltpu.VMEM((R // 2, block_units, sub, wide), bf16),
            pltpu.VMEM((2, sub, wide), f32),
            pltpu.VMEM((stat_rows, cols), f32),
            pltpu.VMEM((R, stat_rows, cols), f32),
            dma((2,)),
            dma((2, units)),
            dma((units,)),
            dma((units,)),
            dma((units,)),
            dma((R // 2, block_units)),
            dma((R,)),
            dma((R,)),
        ],
        compiler_params=pltpu.CompilerParams(
            collective_id=0, has_side_effects=True, vmem_limit_bytes=VMEM_LIMIT
        ),
    )(tokens.reshape(S, sub, features), frozen_weight, at, input_factor, bp)


def reduce_kernel(axes, sizes, with_rows, *refs):
    if with_rows:
        x, rows_ref, out, rows_out, inbox, s1, r1, s2, r2, rsend, rrecv = refs
    else:
        x, out, inbox, s1, r1, s2, r2 = refs
    first, second = axes
    n1, n2 = sizes
    g = n1 * n2
    me = lax.axis_index(first) * n2 + lax.axis_index(second)

    def device(i):
        peer = (me + i) % g
        return {first: peer // n2, second: peer % n2}

    barrier = pltpu.get_barrier_semaphore()

    def loop(body):
        def step(i, carry):
            body(i)
            return carry

        lax.fori_loop(1, g, step, 0)

    loop(lambda i: pl.semaphore_signal(barrier, inc=1, device_id=device(i), device_id_type=MESH))
    pl.semaphore_wait(barrier, g - 1)

    def scatter(i):
        return pltpu.make_async_remote_copy(
            src_ref=x.at[(me + i) % g], dst_ref=inbox.at[i], send_sem=s1.at[i], recv_sem=r1.at[i],
            device_id=device(i), device_id_type=MESH,
        )

    def spread(i, piece):
        return pltpu.make_async_remote_copy(
            src_ref=out.at[piece], dst_ref=out.at[piece], send_sem=s2.at[i], recv_sem=r2.at[i],
            device_id=device(i), device_id_type=MESH,
        )

    loop(lambda i: scatter(i).start())
    if with_rows:
        mine = lax.axis_index(second)

        def row_copy(i, piece):
            return pltpu.make_async_remote_copy(
                src_ref=rows_ref, dst_ref=rows_out.at[piece], send_sem=rsend.at[i],
                recv_sem=rrecv.at[i], device_id={second: (mine + i) % n2}, device_id_type=MESH,
            )

        for i in range(1, n2):
            row_copy(i, mine).start()
        rows_out[mine] = rows_ref[...]

    def gathered(i, total):
        scatter(i).wait_recv()
        return total + inbox[i]

    out[me] = lax.fori_loop(1, g, gathered, x[me])
    loop(lambda i: spread(i, me).start())
    loop(lambda i: spread(i, (me - i + g) % g).wait_recv())
    if with_rows:
        for i in range(1, n2):
            row_copy(i, (mine - i + n2) % n2).wait_recv()
        for i in range(1, n2):
            row_copy(i, mine).wait_send()
    loop(lambda i: scatter(i).wait_send())
    loop(lambda i: spread(i, me).wait_send())


def group_sum(value, axes, identity, rows=None):
    sizes = tuple(lax.axis_size(name) for name in axes)
    g = sizes[0] * sizes[1]
    shape = value.shape
    x = value.reshape(g, -1, LANES)
    vmem = pl.BlockSpec(memory_space=pltpu.VMEM)
    dma = pltpu.SemaphoreType.DMA
    out_shape = [jax.ShapeDtypeStruct(x.shape, jnp.float32)]
    operands = [x]
    scratch = [pltpu.VMEM(x.shape, jnp.float32)] + [dma((g,))] * 4
    if rows is not None:
        out_shape.append(jax.ShapeDtypeStruct((sizes[1],) + rows.shape, jnp.float32))
        operands.append(rows)
        scratch += [dma((sizes[1],))] * 2
    results = pl.pallas_call(
        functools.partial(reduce_kernel, axes, sizes, rows is not None),
        out_shape=tuple(out_shape),
        in_specs=[vmem] * len(operands),
        out_specs=tuple([vmem] * len(out_shape)),
        scratch_shapes=scratch,
        compiler_params=pltpu.CompilerParams(collective_id=identity, has_side_effects=True),
    )(*operands)
    total = results[0].reshape(shape)
    return total if rows is None else (total, results[1])


def per_device(
    tokens,
    frozen_weight,
    input_adapter_factor,
    output_adapter_factor,
    magnitude,
    cotangent,
    sequence_lengths,
):
    row_index = lax.axis_index("row")
    group_index = lax.axis_index("dp")
    block_rows, cols = cotangent.shape
    features = tokens.shape[1]
    rank = input_adapter_factor.shape[0]
    summed, portion, stats = gather_project(
        tokens, frozen_weight, input_adapter_factor, output_adapter_factor
    )
    summed = summed.reshape(block_rows, cols + LANES)
    portion = portion.reshape(-1, features)
    merged_input_factor, norm_sq = stats[:rank], stats[rank]
    down_activations = summed[:, cols:cols + rank].astype(jnp.bfloat16)
    col_norm = jnp.sqrt(norm_sq + norm_eps)
    col_scale = magnitude / col_norm
    query_projection = summed[:, :cols] + jnp.dot(
        down_activations, output_adapter_factor, preferred_element_type=jnp.float32
    )
    projected = (query_projection * col_scale[None, :]).astype(jnp.bfloat16)
    lengths = sequence_lengths[0]
    ends = jnp.cumsum(lengths, dtype=jnp.int32)
    starts = ends - lengths
    positions = row_index * block_rows + jnp.arange(block_rows, dtype=jnp.int32)
    inside = (positions[:, None] >= starts[None, :]) & (positions[:, None] < ends[None, :])
    inverse = 1.0 / lengths.astype(jnp.float32)
    weights = jnp.sum(jnp.where(inside, inverse[None, :], jnp.float32(0.0)), axis=1)
    grad_out = cotangent.astype(jnp.float32) * weights[:, None]
    scale_terms = jnp.sum(grad_out * query_projection, axis=0)
    projection_gradient = (grad_out * col_scale[None, :]).astype(jnp.bfloat16)
    bgrad_terms = contract_product(down_activations, projection_gradient, 0, 0)
    backward_terms = contract_product(output_adapter_factor, projection_gradient, 1, 1)
    terms = jnp.concatenate([bgrad_terms, jnp.pad(scale_terms[None, :], ((0, 7), (0, 0)))], axis=0)
    terms, backward_rows = group_sum(terms, ("dp", "row"), 1, backward_terms)
    bgrad_data, scale_grad = terms[:rank], terms[rank]
    grad_mag = scale_grad / col_norm
    norm_coefficient = -scale_grad * magnitude / (col_norm * col_norm * col_norm)
    grad_b = bgrad_data + merged_input_factor * norm_coefficient[None, :]
    backward = backward_rows.transpose(1, 0, 2).reshape(rank, -1).astype(jnp.bfloat16)
    row_term = jnp.dot(backward, portion, preferred_element_type=jnp.float32)
    scaled_output_factor = (
        output_adapter_factor.astype(jnp.float32) * norm_coefficient[None, :]
    ).astype(jnp.bfloat16)
    norm_term = contract_product(scaled_output_factor, frozen_weight, 1, 1) + jnp.dot(
        contract_product(scaled_output_factor, output_adapter_factor, 1, 1),
        input_adapter_factor.astype(jnp.float32),
        precision=highest_precision,
    )
    first_group = (group_index == 0).astype(jnp.float32)
    input_factor_gradient = group_sum(row_term + first_group * norm_term, ("dp", "col"), 2)
    return (projected, grad_mag, input_factor_gradient, grad_b)


def solution(mesh):
    in_specs = (
        P(("dp", "col"), "row"),
        P("row", "col"),
        P(None, "row"),
        P(None, "col"),
        P("col"),
        P(("dp", "row"), "col"),
        P("dp", None),
    )
    out_specs = (P(("dp", "row"), "col"), P("col"), P(None, "row"), P(None, "col"))
    return jax.shard_map(
        per_device, mesh=mesh, in_specs=in_specs, out_specs=out_specs, check_vma=False
    )
```

time: 367 us -> 142 us (0.39)
  waiting for transfers between devices: 217 us -> 0 us
  Pallas kernels: 0 us -> 114 us
  blocking collectives: 87.8 us -> 0 us
  matrix products: 42.5 us -> 14.5 us
  between operations: 14.3 us -> 0.74 us
  local copies, waits for them, and re-layouts: 1.64 us -> 7.67 us
    psum x3 -> x0, waiting for transfers between devices: 131 us -> none  [the longest x1 71.9 us: per_device(): lax.psum(row_term + first_group * norm_term, ('dp', 'col'))]
    pallas_call x0 -> x3, Pallas kernels: none -> 114 us  [the longest x1 80.5 us: gather_project(): pl.pallas_call(functools.partial(project_kernel, C, R, S), out_shape=(jax...]
    psum x3 -> x0, blocking collectives: 87.8 us -> none  [the longest x1 69.2 us: per_device(): backward_rows = lax.psum(padded, ('row', 'col')).astype(jnp.bfloat16)]
    all_gather x1 -> x0, waiting for transfers between devices: 85.1 us -> none  [per_device(): portion = lax.all_gather(tokens, 'col', axis=0, tiled=True)]
    dot_general x3 -> x1, matrix products: 19.9 us -> 2.84 us  [per_device(): row_term = jnp.dot(backward, portion, preferred_element_type=jnp.float32)]
    dot_general x8 -> x4, matrix products: 19.1 us -> 8.23 us  [contract_product(): lax.dot_general(left, right, (((left_dim,), (right_dim,)), ((), ())), pre...]
    reshape x0 -> x4, local copies, waits for them, and re-layouts: none -> 3.94 us  [the longest x2 2.55 us: group_sum(): total = results[0].reshape(shape)]
  transfers between devices with their start and end apart: 6 -> 0, of which waited for: 4 -> 0; matrix products, arithmetic and copies ran while one was open for 11% -> 0% of each run, Pallas kernels for 0% -> 0%
where the time goes in v1:
time: 142 us
  Pallas kernels  114 us (80%)
  matrix products  14.5 us (10%)
  local copies, waits for them, and re-layouts  7.67 us (5%)
  other arithmetic  5.26 us (4%)
    pallas_call x1, Pallas kernels, gather_project(): pl.pallas_call(functools.partial(project_kernel, C, R, S), out_shape=(jax...  80.5 us
    pallas_call x2, Pallas kernels, group_sum(): pl.pallas_call(functools.partial(reduce_kernel, axes, sizes, rows is not...  33.1 us
    dot_general x4, matrix products, contract_product(): lax.dot_general(left, right, (((left_dim,), (right_dim,)), ((), ())), pre...  8.23 us
    dot_general x1, matrix products, per_device(): jnp.dot(down_activations, output_adapter_factor, preferred_element_type=j...  3.24 us
    dot_general x1, matrix products, per_device(): row_term = jnp.dot(backward, portion, preferred_element_type=jnp.float32)  2.84 us

profile of v1, /device:TPU:0, one launch (start us, length us, event | category | flops | bytes accessed | tf_op | source)
XLA Modules:
  0.0 141.8 jit_solution(10294901425496990819)
XLA Ops:
  0.6 0.7 divide_bitcast_fusion
  1.3 0.8 reduce-window.4
  2.1 0.7 fusion.8
  2.8 0.1 select_reduce_fusion
  2.9 1.1 copy.14
  4.0 0.9 pad.12.at_hbm
  4.9 1.7 %pad.13.b_ref = bf16[128,2048]{1,0:T(8,128)(2,1)} pad(bf16[16,2048]{1,0:T(8,128)(2,1)} %param.10, bf16[]{:T(256)} %constant.8.clone.1), padding=0_112x0_0 | pad | bytes 589826 | tf_op jit(solution)/shard_map/jit(_pad)/pad | solution.py:274
  6.6 0.0 copy-start.3
  6.6 0.0 copy-start
  6.6 0.0 copy-start.4
  6.6 80.5 %shard_map.102 = (f32[4,64,2176]{2,1,0:T(8,128)}, bf16[16,64,2048]{2,1,0:T(8,128)(2,1)}, f32[24,2048]{1,0:T(8,128)}) custom-call(bf16[4,64,2048]{2,1,0:T(8,128)(2,1)} %bitcast.33, bf16[2048,2048]{1,0:T(8,128)(2,1)} %w_hbm.1, bf16[2048,128]{1,0:T(8,128)(2,1)} %pad.12.at_hbm, bf16[16,2048]{1,0:T(8,128)(2,1)} %a_ref.1, bf16[128,2048]{1,0:T(8,128)(2,1)} %pad.13.b_ref), custom_call_target="tpu_custom_call" | custom-call | tf_op jit(solution)/shard_map/pallas_call | solution.py:279
  87.1 0.9 add_sqrt_fusion
  88.0 0.0 copy-done.3
  88.0 0.0 copy-done
  88.0 0.0 copy-done.4
  88.0 3.2 %multiply_reduce_fusion = (f32[2048]{0:T(1024)S(1)}, bf16[256,2048]{1,0:T(8,128)(2,1)}) fusion(bf16[256,2048]{1,0:T(8,128)(2,1)S(1)} %copy-done.4, f32[256]{0:T(256)S(1)} %select_reduce_fusion, f32[2048]{0:T(1024)S(1)} %div.13, bf16[16,2048]{1,0:T(8,128)(2,1)S(1)} %copy-done, f32[256,2176]{1,0:T(8,128)} %bitcast.40), kind=kOutput, calls=%fused_computation.4 | convolution fusion | flops 20449280 | bytes 4408320 | tf_op jit(solution)/shard_map/dot_general | solution.py:429
  91.2 1.3 fusion.2
  92.6 0.7 reshape.55.refs_0_
  93.3 1.1 convolution_bitcast_fusion.refs_1_
  94.4 17.3 %shard_map.103 = (f32[8,48,128]{2,1,0:T(8,128)}, f32[4,16,256]{2,1,0:T(8,128)}) custom-call(f32[8,48,128]{2,1,0:T(8,128)} %reshape.55.refs_0_, f32[16,256]{1,0:T(8,128)} %convolution_bitcast_fusion.refs_1_), custom_call_target="tpu_custom_call" | custom-call | tf_op jit(solution)/shard_map/pallas_call | solution.py:394
  111.7 1.0 reshape.56
  112.7 0.6 fusion.7
  113.3 0.8 convert_bitcast_fusion
  114.1 2.8 %fusion.9 = f32[16,2048]{1,0:T(8,128)S(1)} fusion(bf16[16,1024]{1,0:T(8,128)(2,1)S(1)} %bitcast.34, bf16[1024,2048]{1,0:T(8,128)(2,1)} %bitcast.31), kind=kOutput, calls=%fused_computation.28 | convolution fusion | flops 67108864 | bytes 4358144 | tf_op jit(solution)/shard_map/dot_general | solution.py:452
  117.0 0.0 copy-start.1
  117.0 0.0 copy-start.2
  117.0 5.7 %fusion.4 = f32[16,2048]{1,0:T(8,128)S(1)} fusion(bf16[2048,2048]{1,0:T(8,128)(2,1)} %w_hbm.1, bf16[16,2048]{1,0:T(8,128)(2,1)S(1)} %copy-done, f32[2048]{0:T(1024)S(1)} %get-tuple-element.16), kind=kOutput, calls=%fused_computation.16 | convolution fusion | flops 134316032 | bytes 8593408 | tf_op jit(solution)/shard_map/dot_general | solution.py:18
  122.7 0.1 fusion.3
  122.8 0.0 copy-done.1
  122.8 0.2 fusion.1
  123.1 0.7 reshape.58.refs_0_
  123.7 15.7 %shard_map.104 = f32[8,32,128]{2,1,0:T(8,128)} custom-call(f32[8,32,128]{2,1,0:T(8,128)} %reshape.58.refs_0_), custom_call_target="tpu_custom_call" | custom-call | tf_op jit(solution)/shard_map/pallas_call | solution.py:394
  139.5 1.6 %reshape.59 = f32[16,2048]{1,0:T(8,128)} reshape(f32[8,32,128]{2,1,0:T(8,128)} %shard_map.104) | data formatting | bytes 262144 | tf_op jit(solution)/shard_map/reshape | solution.py:402
  141.1 0.0 copy-done.2
  141.1 0.7 slice_add_fusion
  (5 shorter events, 0.0 us)
Async XLA Ops:
  6.6 81.4 %copy-start.3 = (f32[2048]{0:T(1024)S(1)}, f32[2048]{0:T(1024)}, u32[]{:S(2)}) copy-start(f32[2048]{0:T(1024)} %param.11) | copy-start | bytes 24580
  6.6 81.4 %copy-start = (bf16[16,2048]{1,0:T(8,128)(2,1)S(1)}, bf16[16,2048]{1,0:T(8,128)(2,1)}, u32[]{:S(2)}) copy-start(bf16[16,2048]{1,0:T(8,128)(2,1)} %param.10) | copy-start | bytes 196612
  6.6 81.4 %copy-start.4 = (bf16[256,2048]{1,0:T(8,128)(2,1)S(1)}, bf16[256,2048]{1,0:T(8,128)(2,1)}, u32[]{:S(2)}) copy-start(bf16[256,2048]{1,0:T(8,128)(2,1)} %param.12) | copy-start | bytes 3145732
  117.0 5.8 %copy-start.1 = (bf16[16,2048]{1,0:T(8,128)(2,1)S(1)}, bf16[16,2048]{1,0:T(8,128)(2,1)}, u32[]{:S(2)}) copy-start(bf16[16,2048]{1,0:T(8,128)(2,1)} %a_ref.1) | copy-start | bytes 196612
  117.0 24.1 %copy-start.2 = (f32[24,2048]{1,0:T(8,128)S(1)}, f32[24,2048]{1,0:T(8,128)}, u32[]{:S(2)}) copy-start(f32[24,2048]{1,0:T(8,128)} %get-tuple-element.10) | copy-start | bytes 589828

commit v2 on v0

v2 whole, which is shorter than its diff:
```python
import functools

import jax
import jax.numpy as jnp
from jax import lax
from jax.experimental import pallas as pl
from jax.experimental.pallas import tpu as pltpu
from jax.sharding import PartitionSpec as P

norm_eps = 1e-06
highest_precision = lax.Precision.HIGHEST
MESH = pl.DeviceIdType.MESH
LANES = 128
VMEM_LIMIT = 60 * 1024 * 1024


def contract_product(left, right, left_dim, right_dim):
    return lax.dot_general(
        left, right, (((left_dim,), (right_dim,)), ((), ())), preferred_element_type=jnp.float32
    )


def column_tiles(width, tile):
    return [(start, min(tile, width - start)) for start in range(0, width, tile)]


def adapter_kernel(
    D, C, R, S,
    tok, w_hbm, a_ref, b_ref, magnitude, cot_hbm, lengths,
    projected, grad_mag, factor_grad, grad_b,
    wx, gath, sb, pin, xin, pb, st_in, apad, bpad, acc, pg, cot, row_weight, down_all,
    scale_in, back_in, bsum, bsum_all, box1, fsum, box2,
    load_sem, gsend, grecv, ssend, precv, xrecv, stsend, strecv,
    sc_send, sc_recv, bk_send, bk_recv, r1a, r1b, r1c, r1d, r2a, r2b, r2c, r2d,
):
    z = lax.axis_index("col")
    r = lax.axis_index("row")
    d = lax.axis_index("dp")
    p, q = r // 2, r % 2
    pairs = R // 2
    sub, features = tok.shape[1], tok.shape[2]
    cols = w_hbm.shape[1]
    rank_rows = a_ref.shape[0]
    units = C * S
    block_units = units // R
    block_rows = block_units * sub
    tiles = column_tiles(cols, 512)
    feature_tiles = column_tiles(features, 512)
    f32, bf16 = jnp.float32, jnp.bfloat16

    load_w = pltpu.make_async_copy(w_hbm, wx, load_sem.at[0])
    load_c = pltpu.make_async_copy(cot_hbm, cot, load_sem.at[1])
    load_w.start()
    load_c.start()

    g1, g2 = D * R, D * C
    me1, me2 = d * R + r, d * C + z

    def device1(i):
        peer = (me1 + i) % g1
        return {"dp": peer // R, "row": peer % R}

    def device2(i):
        peer = (me2 + i) % g2
        return {"dp": peer // C, "col": peer % C}

    def loop(n, body):
        def turn(i, carry):
            body(i)
            return carry

        lax.fori_loop(1, n, turn, 0)

    barrier = pltpu.get_barrier_semaphore()
    loop(g1, lambda i: pl.semaphore_signal(barrier, inc=1, device_id=device1(i), device_id_type=MESH))
    loop(g2, lambda i: pl.semaphore_signal(barrier, inc=1, device_id=device2(i), device_id_type=MESH))
    pl.semaphore_wait(barrier, g1 + g2 - 2)

    def hop(src, u, direction):
        target = z - 1 if direction == 0 else z + 1
        return pltpu.make_async_remote_copy(
            src_ref=src, dst_ref=gath.at[u], send_sem=gsend.at[direction, u],
            recv_sem=grecv.at[u], device_id={"col": target}, device_id_type=MESH,
        )

    for s in range(S):
        @pl.when(z > 0)
        def _():
            hop(tok.at[s], z * S + s, 0).start()

        @pl.when(z < C - 1)
        def _():
            hop(tok.at[s], z * S + s, 1).start()

    a = a_ref[...]
    apad[...] = jnp.zeros_like(apad)
    bpad[...] = jnp.zeros_like(bpad)
    apad[0:rank_rows, :] = a
    bpad[0:rank_rows, :] = b_ref[...]
    position = r * block_rows + lax.broadcasted_iota(jnp.int32, (block_rows, LANES), 0)
    weights = jnp.zeros((block_rows, LANES), f32)
    start_row = 0
    for i in range(lengths.shape[1]):
        length = lengths[0, i]
        end_row = start_row + length
        inverse = 1.0 / jnp.full((1, LANES), length, jnp.int32).astype(f32)
        weights = jnp.where((position >= start_row) & (position < end_row), inverse, weights)
        start_row = end_row
    row_weight[...] = weights

    load_w.wait()
    load_c.wait()

    gram = contract_product(a, a, 1, 1)
    for start, width in tiles:
        span = pl.ds(start, width)
        st_in[r, 0:rank_rows, span] = jnp.dot(
            a, wx[:, span], preferred_element_type=f32
        ) + jnp.dot(
            gram, b_ref[:, span].astype(f32),
            precision=highest_precision, preferred_element_type=f32,
        )
        st_in[r, rank_rows:rank_rows + 8, span] = jnp.zeros((8, width), f32)
    depth = 256

    def norm_step(i, carry):
        rows = pl.ds(pl.multiple_of(i * depth, depth), depth)
        for start, width in tiles:
            span = pl.ds(start, width)
            merged = wx[rows, span].astype(f32) + contract_product(apad[:, rows], bpad[:, span], 0, 0)
            st_in[r, rank_rows:rank_rows + 1, span] += jnp.sum(merged * merged, axis=0, keepdims=True)
        return carry

    lax.fori_loop(0, features // depth, norm_step, 0)

    def stat_copy(i, piece):
        return pltpu.make_async_remote_copy(
            src_ref=st_in.at[piece], dst_ref=st_in.at[piece], send_sem=stsend.at[i],
            recv_sem=strecv.at[i], device_id={"row": (r + i) % R}, device_id_type=MESH,
        )

    near = jnp.minimum(z, C - 1 - z)

    def place(k):
        j = k - S
        both = j < 2 * near * S
        rest = j - 2 * near * S
        distance = jnp.where(both, j // (2 * S) + 1, near + 1 + rest // S)
        s = jnp.where(both, (j % (2 * S)) // 2, rest % S)
        leftward = jnp.where(both, j % 2 == 0, z > C - 1 - z)
        chunk = jnp.where(leftward, z - distance, z + distance)
        own = k < S
        return jnp.where(own, z, chunk), jnp.where(own, k, s)

    def pair_copy(u):
        return pltpu.make_async_remote_copy(
            src_ref=sb.at[u], dst_ref=pin.at[u], send_sem=ssend.at[u], recv_sem=precv.at[u],
            device_id={"row": p * 2 + (1 - q)}, device_id_type=MESH,
        )

    def far_copy(u, owner_pair):
        return pltpu.make_async_remote_copy(
            src_ref=sb.at[u], dst_ref=xin.at[p, u % block_units], send_sem=ssend.at[u],
            recv_sem=xrecv.at[p, u % block_units],
            device_id={"row": owner_pair * 2 + q}, device_id_type=MESH,
        )

    def multiply(k):
        c, s = place(k)
        u = c * S + s
        owner = u // block_units

        @pl.when(k < S)
        def _():
            gath[u] = tok[s]

        @pl.when(k >= S)
        def _():
            hop(gath.at[u], u, 0).wait_recv()

            @pl.when((c < z) & (z < C - 1))
            def _():
                hop(gath.at[u], u, 1).start()

            @pl.when((c > z) & (z > 0))
            def _():
                hop(gath.at[u], u, 0).start()

        slot = k % 2
        for start, width in tiles:
            span = pl.ds(start, width)
            pb[slot, :, span] = jnp.dot(gath[u], wx[:, span], preferred_element_type=f32)
        pb[slot, :, pl.ds(cols, LANES)] = contract_product(gath[u], apad[...], 1, 1)

        @pl.when(owner % 2 != q)
        def _():
            sb[u] = pb[slot].astype(bf16)
            pair_copy(u).start()

    def combine(k):
        c, s = place(k)
        u = c * S + s
        owner = u // block_units
        slot = k % 2

        @pl.when(owner % 2 == q)
        def _():
            pair_copy(u).wait_recv()
            total = pb[slot] + pin[u].astype(f32)

            @pl.when(owner // 2 == p)
            def _():
                acc[u % block_units] = total

            @pl.when(owner // 2 != p)
            def _():
                sb[u] = total.astype(bf16)
                far_copy(u, owner // 2).start()

    def step(k, carry):
        @pl.when(k < units)
        def _():
            multiply(k)

        @pl.when(k == 0)
        def _():
            for i in range(1, R):
                stat_copy(i, r).start()

        @pl.when(k > 0)
        def _():
            combine(k - 1)

        return carry

    lax.fori_loop(0, units + 1, step, 0)

    for i in range(1, R):
        stat_copy(i, (r - i + R) % R).wait_recv()
    stats = st_in[0]
    for i in range(1, R):
        stats = stats + st_in[i]
    merged_factor = stats[0:rank_rows]
    col_norm = jnp.sqrt(stats[rank_rows:rank_rows + 1] + norm_eps)
    col_scale = magnitude[...] / col_norm
    scale_in[me1] = jnp.zeros((1, cols), f32)

    def finish(v, carry):
        for i in range(1, pairs):
            other = (p + i) % pairs
            pltpu.make_async_remote_copy(
                src_ref=sb.at[v], dst_ref=xin.at[other, v], send_sem=ssend.at[v],
                recv_sem=xrecv.at[other, v], device_id={"row": other * 2 + q}, device_id_type=MESH,
            ).wait_recv()
            acc[v] += xin[other, v].astype(f32)
        rows = pl.ds(pl.multiple_of(v * sub, sub), sub)
        down = acc[v, :, pl.ds(cols, LANES)].astype(bf16)
        down_all[rows, :] = down
        weight = row_weight[rows, 0:1]
        for start, width in tiles:
            span = pl.ds(start, width)
            scale = col_scale[:, start:start + width]
            query = acc[v, :, span] + jnp.dot(down, bpad[:, span], preferred_element_type=f32)
            projected[rows, span] = (query * scale).astype(bf16)
            grad_out = cot[rows, span].astype(f32) * weight
            scale_in[me1, :, span] += jnp.sum(grad_out * query, axis=0, keepdims=True)
            pg[rows, span] = (grad_out * scale).astype(bf16)
        return carry

    lax.fori_loop(0, block_units, finish, 0)

    def scale_copy(i, piece):
        return pltpu.make_async_remote_copy(
            src_ref=scale_in.at[piece], dst_ref=scale_in.at[piece], send_sem=sc_send.at[i],
            recv_sem=sc_recv.at[i], device_id=device1(i), device_id_type=MESH,
        )

    def back_copy(i, piece):
        return pltpu.make_async_remote_copy(
            src_ref=back_in.at[piece], dst_ref=back_in.at[piece], send_sem=bk_send.at[i],
            recv_sem=bk_recv.at[i], device_id={"row": (r + i) % R}, device_id_type=MESH,
        )

    back_in[r] = contract_product(b_ref[...], pg[...], 1, 1).astype(bf16)
    loop(g1, lambda i: scale_copy(i, me1).start())
    for i in range(1, R):
        back_copy(i, r).start()

    def group_sum(g, me, device, src, box, out, s1, r1, s2, r2):
        width = max(LANES, src.shape[1] // g)
        pieces = src.shape[1] // width

        def part(j):
            return pl.ds(pl.multiple_of(j * width, width), width)

        def scatter(i):
            return pltpu.make_async_remote_copy(
                src_ref=src.at[:, part((me + i) % g % pieces)], dst_ref=box.at[i],
                send_sem=s1.at[i], recv_sem=r1.at[i], device_id=device(i), device_id_type=MESH,
            )

        def spread(i, j):
            return pltpu.make_async_remote_copy(
                src_ref=out.at[:, part(j % pieces)], dst_ref=out.at[:, part(j % pieces)],
                send_sem=s2.at[i], recv_sem=r2.at[i], device_id=device(i), device_id_type=MESH,
            )

        def to_owner(i, action):
            @pl.when((me + i) % g < pieces)
            def _():
                action(scatter(i))

        def from_owner(i, action):
            @pl.when((me - i + g) % g < pieces)
            def _():
                action(spread(i, (me - i + g) % g))

        def begin():
            loop(g, lambda i: to_owner(i, lambda copy: copy.start()))

        def middle():
            @pl.when(me < pieces)
            def _():
                def add(i, total):
                    scatter(i).wait_recv()
                    return total + box[i]

                out[:, part(me % pieces)] = lax.fori_loop(1, g, add, src[:, part(me % pieces)])
                loop(g, lambda i: spread(i, me).start())

        def end():
            loop(g, lambda i: from_owner(i, lambda copy: copy.wait_recv()))

        def drain():
            loop(g, lambda i: to_owner(i, lambda copy: copy.wait_send()))

            @pl.when(me < pieces)
            def _():
                loop(g, lambda i: spread(i, me).wait_send())

        return begin, middle, end, drain

    begin1, middle1, end1, drain1 = group_sum(
        g1, me1, device1, bsum, box1, bsum_all, r1a, r1b, r1c, r1d
    )
    begin2, middle2, end2, drain2 = group_sum(
        g2, me2, device2, fsum, box2, factor_grad, r2a, r2b, r2c, r2d
    )
    for start, width in tiles:
        span = pl.ds(start, width)
        bsum[:, span] = contract_product(down_all[...], pg[:, span], 0, 0)[0:rank_rows]
    begin1()

    for i in range(1, R):
        back_copy(i, (r - i + R) % R).wait_recv()
    for start, width in feature_tiles:
        span = pl.ds(start, width)
        term = jnp.zeros((rank_rows, width), f32)
        for j in range(R):
            block = gath[j * block_units:(j + 1) * block_units, :, span].reshape(block_rows, width)
            term = term + jnp.dot(back_in[j], block, preferred_element_type=f32)
        fsum[:, span] = term

    loop(g1, lambda i: scale_copy(i, (me1 - i + g1) % g1).wait_recv())
    scale_grad = scale_in[0]
    for j in range(1, g1):
        scale_grad = scale_grad + scale_in[j]
    grad_mag[...] = scale_grad / col_norm
    coefficient = -scale_grad * magnitude[...] / (col_norm * col_norm * col_norm)
    scaled = (b_ref[...].astype(f32) * coefficient).astype(bf16)
    cross = contract_product(scaled, b_ref[...], 1, 1)
    for index, (start, width) in enumerate(feature_tiles):
        @pl.when(d == index % D)
        def _():
            span = pl.ds(start, width)
            fsum[:, span] += contract_product(scaled, wx[span, :], 1, 1) + jnp.dot(
                cross, a_ref[:, span].astype(f32),
                precision=highest_precision, preferred_element_type=f32,
            )
    begin2()
    middle1()
    middle2()
    end1()
    grad_b[...] = bsum_all[...] + merged_factor * coefficient
    end2()

    drain1()
    drain2()
    loop(g1, lambda i: scale_copy(i, me1).wait_send())
    for i in range(1, R):
        stat_copy(i, r).wait_send()
        back_copy(i, r).wait_send()

    def drain(u, carry):
        c = u // S
        owner = u // block_units

        @pl.when((owner % 2 != q) | (owner // 2 != p))
        def _():
            pair_copy(u).wait_send()

        @pl.when((c <= z) & (z < C - 1))
        def _():
            hop(gath.at[u], u, 1).wait_send()

        @pl.when((c >= z) & (z > 0))
        def _():
            hop(gath.at[u], u, 0).wait_send()

        return carry

    lax.fori_loop(0, units, drain, 0)


def per_device(
    tokens,
    frozen_weight,
    input_adapter_factor,
    output_adapter_factor,
    magnitude,
    cotangent,
    sequence_lengths,
):
    D, C, R = lax.axis_size("dp"), lax.axis_size("col"), lax.axis_size("row")
    local_rows, features = tokens.shape
    block_rows, cols = cotangent.shape
    rank_rows = input_adapter_factor.shape[0]
    S = 4
    sub = local_rows // S
    units = C * S
    block_units = units // R
    wide = cols + LANES
    g1, g2 = D * R, D * C
    vmem = pl.BlockSpec(memory_space=pltpu.VMEM)
    smem = pl.BlockSpec(memory_space=pltpu.SMEM)
    hbm = pl.BlockSpec(memory_space=pl.ANY)
    dma = pltpu.SemaphoreType.DMA
    f32, bf16 = jnp.float32, jnp.bfloat16
    projected, grad_mag, factor_grad, grad_b = pl.pallas_call(
        functools.partial(adapter_kernel, D, C, R, S),
        out_shape=(
            jax.ShapeDtypeStruct((block_rows, cols), bf16),
            jax.ShapeDtypeStruct((1, cols), f32),
            jax.ShapeDtypeStruct((rank_rows, features), f32),
            jax.ShapeDtypeStruct((rank_rows, cols), f32),
        ),
        in_specs=[vmem, hbm, vmem, vmem, vmem, hbm, smem],
        out_specs=(vmem, vmem, vmem, vmem),
        scratch_shapes=[
            pltpu.VMEM((features, cols), bf16),
            pltpu.VMEM((units, sub, features), bf16),
            pltpu.VMEM((units, sub, wide), bf16),
            pltpu.VMEM((units, sub, wide), bf16),
            pltpu.VMEM((R // 2, block_units, sub, wide), bf16),
            pltpu.VMEM((2, sub, wide), f32),
            pltpu.VMEM((R, rank_rows + 8, cols), f32),
            pltpu.VMEM((LANES, features), bf16),
            pltpu.VMEM((LANES, cols), bf16),
            pltpu.VMEM((block_units, sub, wide), f32),
            pltpu.VMEM((block_rows, cols), bf16),
            pltpu.VMEM((block_rows, cols), bf16),
            pltpu.VMEM((block_rows, LANES), f32),
            pltpu.VMEM((block_rows, LANES), bf16),
            pltpu.VMEM((g1, 1, cols), f32),
            pltpu.VMEM((R, rank_rows, block_rows), bf16),
            pltpu.VMEM((rank_rows, cols), f32),
            pltpu.VMEM((rank_rows, cols), f32),
            pltpu.VMEM((g1, rank_rows, max(LANES, cols // g1)), f32),
            pltpu.VMEM((rank_rows, features), f32),
            pltpu.VMEM((g2, rank_rows, max(LANES, features // g2)), f32),
            dma((2,)),
            dma((2, units)),
            dma((units,)),
            dma((units,)),
            dma((units,)),
            dma((R // 2, block_units)),
            dma((R,)),
            dma((R,)),
            dma((g1,)),
            dma((g1,)),
            dma((R,)),
            dma((R,)),
        ] + [dma((g1,))] * 4 + [dma((g2,))] * 4,
        compiler_params=pltpu.CompilerParams(
            collective_id=0, has_side_effects=True, vmem_limit_bytes=VMEM_LIMIT
        ),
    )(
        tokens.reshape(S, sub, features), frozen_weight, input_adapter_factor,
        output_adapter_factor, magnitude.reshape(1, cols), cotangent, sequence_lengths,
    )
    return projected, grad_mag.reshape(cols), factor_grad, grad_b


def solution(mesh):
    in_specs = (
        P(("dp", "col"), "row"),
        P("row", "col"),
        P(None, "row"),
        P(None, "col"),
        P("col"),
        P(("dp", "row"), "col"),
        P("dp", None),
    )
    out_specs = (P(("dp", "row"), "col"), P("col"), P(None, "row"), P(None, "col"))
    return jax.shard_map(
        per_device, mesh=mesh, in_specs=in_specs, out_specs=out_specs, check_vma=False
    )
```

time: 367 us -> 113 us (0.31)
  waiting for transfers between devices: 217 us -> 0 us
  Pallas kernels: 0 us -> 106 us
  blocking collectives: 87.8 us -> 0 us
  matrix products: 42.5 us -> 0 us
  between operations: 14.3 us -> 0.64 us
  local copies, waits for them, and re-layouts: 1.64 us -> 6.73 us
    psum x3 -> x0, waiting for transfers between devices: 131 us -> none  [the longest x1 71.9 us: per_device(): lax.psum(row_term + first_group * norm_term, ('dp', 'col'))]
    pallas_call x0 -> x1, Pallas kernels: none -> 106 us  [per_device(): pl.pallas_call(functools.partial(adapter_kernel, D, C, R, S), out_shape=(...]
    psum x3 -> x0, blocking collectives: 87.8 us -> none  [the longest x1 69.2 us: per_device(): backward_rows = lax.psum(padded, ('row', 'col')).astype(jnp.bfloat16)]
    all_gather x1 -> x0, waiting for transfers between devices: 85.1 us -> none  [per_device(): portion = lax.all_gather(tokens, 'col', axis=0, tiled=True)]
    dot_general x13 -> x0, matrix products: 42.5 us -> none  [the longest x8 19.1 us: contract_product(): lax.dot_general(left, right, (((left_dim,), (right_dim,)), ((), ())), pre...]
    unnamed x13 -> x4, local copies, waits for them, and re-layouts: 1.6 us -> 6.73 us
  transfers between devices with their start and end apart: 6 -> 0, of which waited for: 4 -> 0; matrix products, arithmetic and copies ran while one was open for 11% -> 0% of each run, Pallas kernels for 0% -> 0%
where the time goes in v2:
time: 113 us
  Pallas kernels  106 us (94%)
  local copies, waits for them, and re-layouts  6.73 us (6%)
    pallas_call x1, Pallas kernels, per_device(): pl.pallas_call(functools.partial(adapter_kernel, D, C, R, S), out_shape=(...  106 us
    unnamed x4, local copies, waits for them, and re-layouts  6.73 us

profile of v2, /device:TPU:0, one launch (start us, length us, event | category | flops | bytes accessed | tf_op | source)
XLA Modules:
  0.0 113.0 jit_solution(8170428634691261099)
XLA Ops:
  0.6 105.6 %shard_map.102 = (bf16[256,2048]{1,0:T(8,128)(2,1)}, f32[1,2048]{1,0:T(1,128)}, f32[16,2048]{1,0:T(8,128)}, f32[16,2048]{1,0:T(8,128)}) custom-call(bf16[4,64,2048]{2,1,0:T(8,128)(2,1)} %bitcast.3, bf16[2048,2048]{1,0:T(8,128)(2,1)} %w_hbm.1, bf16[16,2048]{1,0:T(8,128)(2,1)} %a_ref.1, bf16[16,2048]{1,0:T(8,128)(2,1)} %b_ref.1, f32[1,2048]{1,0:T(1,128)} %bitcast.4, ...), custom_call_target="tpu_custom_call" | custom-call | tf_op jit(solution)/shard_map/pallas_call | solution.py:439
  106.2 2.3 %copy.15 = bf16[256,2048]{1,0:T(8,128)(2,1)} copy(bf16[256,2048]{1,0:T(8,128)(2,1)} %get-tuple-element.16) | data formatting | bytes 2097152
  108.6 1.3 %copy.16 = f32[2048]{0:T(1024)} copy(f32[2048]{0:T(1024)} %bitcast.5) | data formatting | bytes 16384
  109.8 1.6 %copy.17 = f32[16,2048]{1,0:T(8,128)} copy(f32[16,2048]{1,0:T(8,128)} %get-tuple-element.18) | data formatting | bytes 262144
  111.4 1.6 %copy.18 = f32[16,2048]{1,0:T(8,128)} copy(f32[16,2048]{1,0:T(8,128)} %get-tuple-element.19) | data formatting | bytes 262144

commit v3 on v2

--- a/solution.py
+++ b/solution.py
@@ -27,8 +27,8 @@
 def adapter_kernel(
     D, C, R, S,
     tok, w_hbm, a_ref, b_ref, magnitude, cot_hbm, lengths,
-    projected, grad_mag, factor_grad, grad_b,
-    wx, gath, sb, pin, xin, pb, st_in, apad, bpad, acc, pg, cot, row_weight, down_all,
+    projected_hbm, grad_mag, factor_grad, grad_b,
+    projected, norm_row, scale_row, fsum_all, wx, gath, sb, pin, xin, pb, st_in, apad, bpad, acc, pg, cot, row_weight, down_all,
     scale_in, back_in, bsum, bsum_all, box1, fsum, box2,
     load_sem, gsend, grecv, ssend, precv, xrecv, stsend, strecv,
     sc_send, sc_recv, bk_send, bk_recv, r1a, r1b, r1c, r1d, r2a, r2b, r2c, r2d,
@@ -217,35 +217,19 @@
                 sb[u] = total.astype(bf16)
                 far_copy(u, owner // 2).start()
 
-    def step(k, carry):
-        @pl.when(k < units)
-        def _():
-            multiply(k)
-
-        @pl.when(k == 0)
-        def _():
-            for i in range(1, R):
-                stat_copy(i, r).start()
-
-        @pl.when(k > 0)
-        def _():
-            combine(k - 1)
-
-        return carry
-
-    lax.fori_loop(0, units + 1, step, 0)
-
-    for i in range(1, R):
-        stat_copy(i, (r - i + R) % R).wait_recv()
-    stats = st_in[0]
-    for i in range(1, R):
-        stats = stats + st_in[i]
-    merged_factor = stats[0:rank_rows]
-    col_norm = jnp.sqrt(stats[rank_rows:rank_rows + 1] + norm_eps)
-    col_scale = magnitude[...] / col_norm
     scale_in[me1] = jnp.zeros((1, cols), f32)
 
-    def finish(v, carry):
+    def prepare():
+        for i in range(1, R):
+            stat_copy(i, (r - i + R) % R).wait_recv()
+        norm_sq = st_in[0, rank_rows:rank_rows + 1]
+        for i in range(1, R):
+            norm_sq = norm_sq + st_in[i, rank_rows:rank_rows + 1]
+        norm = jnp.sqrt(norm_sq + norm_eps)
+        norm_row[...] = norm
+        scale_row[...] = magnitude[...] / norm
+
+    def finish(v):
         for i in range(1, pairs):
             other = (p + i) % pairs
             pltpu.make_async_remote_copy(
@@ -259,15 +243,51 @@
         weight = row_weight[rows, 0:1]
         for start, width in tiles:
             span = pl.ds(start, width)
-            scale = col_scale[:, start:start + width]
+            scale = scale_row[:, span]
             query = acc[v, :, span] + jnp.dot(down, bpad[:, span], preferred_element_type=f32)
             projected[rows, span] = (query * scale).astype(bf16)
             grad_out = cot[rows, span].astype(f32) * weight
             scale_in[me1, :, span] += jnp.sum(grad_out * query, axis=0, keepdims=True)
             pg[rows, span] = (grad_out * scale).astype(bf16)
+
+    lag = min(3, units)
+
+    def step(k, carry):
+        @pl.when(k < units)
+        def _():
+            multiply(k)
+
+        @pl.when(k == 0)
+        def _():
+            for i in range(1, R):
+                stat_copy(i, r).start()
+
+        @pl.when((k > 0) & (k <= units))
+        def _():
+            combine(k - 1)
+
+        @pl.when(k == lag)
+        def _():
+            prepare()
+
+        @pl.when(k >= lag)
+        def _():
+            c, s = place(k - lag)
+            u = c * S + s
+
+            @pl.when(u // block_units == r)
+            def _():
+                finish(u % block_units)
+
         return carry
 
-    lax.fori_loop(0, block_units, finish, 0)
+    lax.fori_loop(0, units + lag, step, 0)
+    leave = pltpu.make_async_copy(projected, projected_hbm, load_sem.at[0])
+    leave.start()
+    col_norm = norm_row[...]
+    merged_factor = st_in[0, 0:rank_rows]
+    for i in range(1, R):
+        merged_factor = merged_factor + st_in[i, 0:rank_rows]
 
     def scale_copy(i, piece):
         return pltpu.make_async_remote_copy(
@@ -325,7 +345,8 @@
                     scatter(i).wait_recv()
                     return total + box[i]
 
-                out[:, part(me % pieces)] = lax.fori_loop(1, g, add, src[:, part(me % pieces)])
+                total = lax.fori_loop(1, g, add, src[:, part(me % pieces)])
+                out[:, part(me % pieces)] = total.astype(out.dtype)
                 loop(g, lambda i: spread(i, me).start())
 
         def end():
@@ -344,7 +365,7 @@
         g1, me1, device1, bsum, box1, bsum_all, r1a, r1b, r1c, r1d
     )
     begin2, middle2, end2, drain2 = group_sum(
-        g2, me2, device2, fsum, box2, factor_grad, r2a, r2b, r2c, r2d
+        g2, me2, device2, fsum, box2, fsum_all, r2a, r2b, r2c, r2d
     )
     for start, width in tiles:
         span = pl.ds(start, width)
@@ -383,6 +404,8 @@
     end1()
     grad_b[...] = bsum_all[...] + merged_factor * coefficient
     end2()
+    factor_grad[...] = fsum_all[...].astype(f32)
+    leave.wait()
 
     drain1()
     drain2()
@@ -410,6 +433,19 @@
         return carry
 
     lax.fori_loop(0, units, drain, 0)
+
+
+def deliver_kernel(*refs):
+    sources, targets, held, loaded, stored = refs[:4], refs[4:8], refs[8:12], refs[12], refs[13]
+    loads = [pltpu.make_async_copy(sources[i], held[i], loaded.at[i]) for i in range(4)]
+    stores = [pltpu.make_async_copy(held[i], targets[i], stored.at[i]) for i in range(4)]
+    for load in loads:
+        load.start()
+    for load, store in zip(loads, stores):
+        load.wait()
+        store.start()
+    for store in stores:
+        store.wait()
 
 
 def per_device(
@@ -445,8 +481,12 @@
             jax.ShapeDtypeStruct((rank_rows, cols), f32),
         ),
         in_specs=[vmem, hbm, vmem, vmem, vmem, hbm, smem],
-        out_specs=(vmem, vmem, vmem, vmem),
+        out_specs=(hbm, vmem, vmem, vmem),
         scratch_shapes=[
+            pltpu.VMEM((block_rows, cols), bf16),
+            pltpu.VMEM((1, cols), f32),
+            pltpu.VMEM((1, cols), f32),
+            pltpu.VMEM((rank_rows, features), bf16),
             pltpu.VMEM((features, cols), bf16),
             pltpu.VMEM((units, sub, features), bf16),
             pltpu.VMEM((units, sub, wide), bf16),
@@ -488,6 +528,17 @@
         tokens.reshape(S, sub, features), frozen_weight, input_adapter_factor,
         output_adapter_factor, magnitude.reshape(1, cols), cotangent, sequence_lengths,
     )
+    projected, grad_mag, factor_grad, grad_b = pl.pallas_call(
+        deliver_kernel,
+        out_shape=tuple(
+            jax.ShapeDtypeStruct(x.shape, x.dtype) for x in (projected, grad_mag, factor_grad, grad_b)
+        ),
+        in_specs=[hbm] * 4,
+        out_specs=(hbm,) * 4,
+        scratch_shapes=[
+            pltpu.VMEM(x.shape, x.dtype) for x in (projected, grad_mag, factor_grad, grad_b)
+        ] + [dma((4,)), dma((4,))],
+    )(projected, grad_mag, factor_grad, grad_b)
     return projected, grad_mag.reshape(cols), factor_grad, grad_b
 
 

time: 113 us -> 117 us (1.035)
  Pallas kernels: 106 us -> 116 us
  local copies, waits for them, and re-layouts: 6.73 us -> 0 us
    pallas_call x1, Pallas kernels: 106 us -> 114 us  [per_device(): pl.pallas_call(functools.partial(adapter_kernel, D, C, R, S), out_shape=(...]
    unnamed x4 -> x0, local copies, waits for them, and re-layouts: 6.73 us -> none
    pallas_call x0 -> x1, Pallas kernels: none -> 2.34 us  [per_device(): pl.pallas_call(deliver_kernel, out_shape=tuple((jax.ShapeDtypeStruct(x.sh...]
where the time goes in v3:
time: 117 us
  Pallas kernels  116 us (99%)
    pallas_call x1, Pallas kernels, per_device(): pl.pallas_call(functools.partial(adapter_kernel, D, C, R, S), out_shape=(...  114 us
    pallas_call x1, Pallas kernels, per_device(): pl.pallas_call(deliver_kernel, out_shape=tuple((jax.ShapeDtypeStruct(x.sh...  2.34 us

profile of v3, /device:TPU:0, one launch (start us, length us, event | category | flops | bytes accessed | tf_op | source)
XLA Modules:
  0.0 116.6 jit_solution(17938874720049776406)
XLA Ops:
  0.6 113.6 %shard_map.102 = (bf16[256,2048]{1,0:T(8,128)(2,1)}, f32[1,2048]{1,0:T(1,128)}, f32[16,2048]{1,0:T(8,128)}, f32[16,2048]{1,0:T(8,128)}) custom-call(bf16[4,64,2048]{2,1,0:T(8,128)(2,1)} %bitcast.3, bf16[2048,2048]{1,0:T(8,128)(2,1)} %w_hbm.1, bf16[16,2048]{1,0:T(8,128)(2,1)} %a_ref.1, bf16[16,2048]{1,0:T(8,128)(2,1)} %b_ref.1, f32[1,2048]{1,0:T(1,128)} %bitcast.4, ...), custom_call_target="tpu_custom_call" | custom-call | tf_op jit(solution)/shard_map/pallas_call | solution.py:475
  114.2 2.3 %shard_map.103 = (bf16[256,2048]{1,0:T(8,128)(2,1)}, f32[1,2048]{1,0:T(1,128)}, f32[16,2048]{1,0:T(8,128)}, f32[16,2048]{1,0:T(8,128)}) custom-call(bf16[256,2048]{1,0:T(8,128)(2,1)} %get-tuple-element.12.refs_0_, f32[1,2048]{1,0:T(1,128)} %get-tuple-element.13.refs_1_, f32[16,2048]{1,0:T(8,128)} %get-tuple-element.14.refs_2_, ...), custom_call_target="tpu_custom_call" | custom-call | tf_op jit(solution)/shard_map/pallas_call | solution.py:531
